TPU v7x, 512 devices: a 4x2x32 block of a 4x8x32 slice. The times are simulated.
512 devices in a mesh: groups: 2 (over y), pix: 32 (over z), sub: 4 (over x), rep: 2 (over core).
Axes of the slice: x: 4, y: 2, z: 32, core: 2. Of those that a mesh axis runs over, the one named last changes fastest.
The devices are a block of a 4x8x32 slice.
Arguments:
- gaia_pos: float32 [2, 65536], P(None, ('groups', 'pix', 'sub', 'rep')), parts along dimension 1, may hold values from 0 to 1
- gaia_shape: float32 [2, 65536], P(None, ('groups', 'pix', 'sub', 'rep')), parts along dimension 1, may hold values from 0.15 to 0.6
- gaia_corr: float32 [65536], P(('groups', 'pix', 'sub', 'rep')), parts along dimension 0, may hold values from -0.8 to 0.8
- gaia_dest: int32 [65536, 1], P(('groups', 'pix', 'sub', 'rep')), parts along dimension 0, may hold values from 0 to 127; in each aligned block of 128 rows (0 to 127, 128 to 255, ...) at most 2 rows name the same one
- gaia_cell: int32 [65536], P(('groups', 'pix', 'sub', 'rep')), parts along dimension 0, may hold values from 0 to 127
- wise_pos: float32 [2, 65536], P(None, ('groups', 'pix', 'sub', 'rep')), parts along dimension 1, may hold values from 0 to 1
- wise_shape: float32 [2, 65536], P(None, ('groups', 'pix', 'sub', 'rep')), parts along dimension 1, may hold values from 0.15 to 0.6
- wise_corr: float32 [65536], P(('groups', 'pix', 'sub', 'rep')), parts along dimension 0, may hold values from -0.8 to 0.8
- wise_dest: int32 [65536, 1], P(('groups', 'pix', 'sub', 'rep')), parts along dimension 0, may hold values from 0 to 127; in each aligned block of 128 rows (0 to 127, 128 to 255, ...) at most 2 rows name the same one
- wise_cell: int32 [65536], P(('groups', 'pix', 'sub', 'rep')), parts along dimension 0, may hold values from 0 to 127
Outputs:
- gaia_like: float32 [65536], P(('groups', 'pix', 'sub', 'rep')), parts along dimension 0
- gaia_offset: float32 [2, 65536], P(None, ('groups', 'pix', 'sub', 'rep')), parts along dimension 1
- wise_like: float32 [65536], P(('groups', 'pix', 'sub', 'rep')), parts along dimension 0
There are 2 independent parts, one for each index of `groups`. A program takes and returns all parts, laid end to end along the dimension named above; each array names one. Nothing has to cross between parts.
Inputs may be any that keep to these rules, and one draw needn't show every extreme that they name: `gaia_dest`: among the 128 sources of one device no target appears more than 2 times, and some target appears exactly 2 times; the owner of a source is dest // 4. `wise_dest`: among the 128 sources of one device no target appears more than 2 times, and some target appears exactly 2 times; the owner of a source is dest // 4. `gaia_cell`: pixel row inside the band is cell // 64, column cell % 64. `wise_cell`: pixel row inside the band is cell // 64, column cell % 64.
All inputs are finite; a program needn't handle non-finite values.
Results may differ from a plain program's by a relative error of at most 0.0003.
Values sent between devices are 32-bit elements; how exact they have to be, the bound alone decides.
No kernel may reach another device: no remote copies, remote signals or barrier semaphores. Data moves between devices by JAX's collectives and lax.ppermute only.
A program may use at most 64 MiB of HBM per device.

v0:
```python
import jax
import jax.numpy as jnp
from jax import lax
from jax.sharding import PartitionSpec as P

SRC_DEV = 128
BAND = 2
NCOL = 64
empty_gaia = -1000.0
empty_wise = -3000.0
row_offset = 4.0
inv_two_pi = 0.15915494309189535


def side_by_side(arrays, axis, split_dim, concat_dim, along):
    ends, at = ([], 0)
    for a in arrays[:-1]:
        at += a.shape[along]
        ends.append(at)
    both = jnp.concatenate(arrays, axis=along)
    return tuple(
        jnp.split(
            lax.all_to_all(both, axis, split_axis=split_dim, concat_axis=concat_dim, tiled=True),
            ends,
            axis=along,
        )
    )


def with_halo(x, sides, width):
    for axis, dim in sides:
        size, length = (lax.axis_size(axis), x.shape[dim])
        up = [(i, (i + 1) % size) for i in range(size - 1)]
        down = [(j, i) for i, j in up]
        last = lax.slice_in_dim(x, length - width, length, axis=dim)
        leading = lax.slice_in_dim(x, 0, width, axis=dim)
        before = lax.ppermute(last, axis, up)
        after = lax.ppermute(leading, axis, down)
        x = jnp.concatenate([before, x, after], axis=dim)
    return x


def from_everyone(x, axis):
    size = lax.axis_size(axis)
    return lax.all_to_all(jnp.broadcast_to(x[None], (size, *x.shape)), axis, 0, 0, tiled=True)


def joined_along(parts, dim):
    parts = jnp.moveaxis(parts, 0, dim)
    shape = parts.shape
    return parts.reshape(*shape[:dim], shape[dim] * shape[dim + 1], *shape[dim + 2 :])


def gathered_copies(x, axis, dim):
    parts = from_everyone(x, axis)
    return joined_along(parts, dim)


def in_blocks(x, dim, size):
    before, after = (x.shape[:dim], x.shape[dim + 1 :])
    return jnp.moveaxis(x.reshape(*before, size, -1, *after), dim, 0)


def sent_and_summed(x, axis, dim):
    size = lax.axis_size(axis)
    parts = lax.all_to_all(in_blocks(x, dim, size), axis, 0, 0, tiled=True)
    return jnp.sum(parts, axis=0)


def from_behind(value, axis, steps):
    count = lax.axis_size(axis)
    leading, last = (max(0, -steps), min(count, count - steps))
    return lax.ppermute(value, axis, [(source, source + steps) for source in range(leading, last)])


def pack_rows(position, shape, corr, dest, cell, sub_count):
    owner = dest // sub_count
    row = owner * BAND + cell // NCOL
    column = cell % NCOL
    axis_x = shape[0]
    axis_y = shape[1]
    return jnp.stack(
        [
            position[0],
            position[1],
            axis_x * axis_x,
            axis_y * axis_y,
            corr * axis_x * axis_y,
            row.astype(jnp.float32) + row_offset,
            column.astype(jnp.float32),
        ]
    )


def empty_rows(width, code):
    base = jnp.zeros((7, width), jnp.float32)
    return base.at[2:4].set(1.0).at[5].set(code)


def pair_terms(gaia, wise):
    row_gap = gaia[5][:, None] - wise[5][None, :]
    col_gap = jnp.mod(gaia[6][:, None] - wise[6][None, :] + 1.0, NCOL) - 1.0
    near = (jnp.abs(row_gap) <= 1.0) & (jnp.abs(col_gap) <= 1.0)
    step_x = col_gap + gaia[0][:, None] - wise[0][None, :]
    step_y = row_gap + gaia[1][:, None] - wise[1][None, :]
    spread_x = gaia[2][:, None] + wise[2][None, :]
    spread_y = gaia[3][:, None] + wise[3][None, :]
    spread_xy = gaia[4][:, None] + wise[4][None, :]
    determinant = spread_x * spread_y - spread_xy * spread_xy
    chi_square = (
        spread_y * step_x * step_x - 2.0 * spread_xy * step_x * step_y + spread_x * step_y * step_y
    ) / determinant
    like = jnp.where(near, jnp.exp(-0.5 * chi_square) * inv_two_pi / jnp.sqrt(determinant), 0.0)
    return (
        jnp.sum(like, axis=1),
        jnp.sum(like * step_x, axis=1),
        jnp.sum(like * step_y, axis=1),
        jnp.sum(like, axis=0),
    )


def slots_of(dest, capacity):
    order = jnp.arange(dest.shape[0], dtype=jnp.int32)
    same = (dest[:, None] == dest[None, :]) & (order[None, :] < order[:, None])
    rank = jnp.sum(same.astype(jnp.int32), axis=1, dtype=jnp.int32)
    return dest * capacity + rank


def fold_columns(rows, block_width, carry, piece):
    row_totals, column_totals = carry
    count = piece.shape[1]
    blocks = piece.reshape(7, count // block_width, block_width).transpose(1, 0, 2)

    def column_step(totals, part):
        like, moment_x, moment_y, column_sums = pair_terms(rows, part)
        return (totals + jnp.stack([like, moment_x, moment_y]), column_sums)

    row_totals, column_sums = lax.scan(column_step, row_totals, blocks)
    column_totals = column_sums.reshape(-1)
    return (row_totals, column_totals)


def shards(
    gaia_pos,
    gaia_shape,
    gaia_corr,
    gaia_dest,
    gaia_cell,
    wise_pos,
    wise_shape,
    wise_corr,
    wise_dest,
    wise_cell,
):
    pix_count = lax.axis_size("pix")
    sub_count = lax.axis_size("sub")
    targets = pix_count * sub_count
    capacity = max(2, 5 * SRC_DEV // (2 * targets))
    received = targets * capacity
    block_width = received // 2
    gaia_rows = pack_rows(gaia_pos, gaia_shape, gaia_corr, gaia_dest[:, 0], gaia_cell, sub_count)
    wise_rows = pack_rows(wise_pos, wise_shape, wise_corr, wise_dest[:, 0], wise_cell, sub_count)
    gaia_slot = slots_of(gaia_dest[:, 0], capacity)
    wise_slot = slots_of(wise_dest[:, 0], capacity)
    gaia_send = empty_rows(received, empty_gaia).at[:, gaia_slot].set(gaia_rows)
    wise_send = empty_rows(received, empty_wise).at[:, wise_slot].set(wise_rows)
    gaia_here, wise_here = side_by_side((gaia_send, wise_send), ("pix", "sub"), 1, 1, 0)
    nearby = with_halo(wise_here, (("pix", 1),), received)
    members = sub_count * lax.axis_size("rep")
    start_totals = (
        jnp.zeros((3, received), jnp.float32),
        jnp.zeros((members * 3 * received,), jnp.float32),
    )
    gaia_result, column_totals = fold_columns(
        gaia_here, block_width, start_totals, gathered_copies(nearby, ("sub", "rep"), 1)
    )
    wise_part = sent_and_summed(column_totals, ("sub", "rep"), 0)
    from_upper = from_behind(wise_part[:received], "pix", -1)
    from_lower = from_behind(wise_part[2 * received :], "pix", 1)
    wise_result = wise_part[received : 2 * received] + from_lower + from_upper
    results = jnp.concatenate([gaia_result, wise_result[None, :]], axis=0)
    returned = lax.all_to_all(results, ("pix", "sub"), split_axis=1, concat_axis=1, tiled=True)
    return (returned[0][gaia_slot], returned[1:3][:, gaia_slot], returned[3][wise_slot])


def solution(mesh):
    return jax.shard_map(
        shards,
        mesh=mesh,
        in_specs=(
            P(None, ("groups", "pix", "sub", "rep")),
            P(None, ("groups", "pix", "sub", "rep")),
            P(("groups", "pix", "sub", "rep")),
            P(("groups", "pix", "sub", "rep"), None),
            P(("groups", "pix", "sub", "rep")),
            P(None, ("groups", "pix", "sub", "rep")),
            P(None, ("groups", "pix", "sub", "rep")),
            P(("groups", "pix", "sub", "rep")),
            P(("groups", "pix", "sub", "rep"), None),
            P(("groups", "pix", "sub", "rep")),
        ),
        out_specs=(
            P(("groups", "pix", "sub", "rep")),
            P(None, ("groups", "pix", "sub", "rep")),
            P(("groups", "pix", "sub", "rep")),
        ),
        check_vma=False,
    )
```

profile of v0, /device:TPU:46, one launch (start us, length us, event | category | flops | bytes accessed | tf_op | source)
XLA Modules:
  0.0 202.2 jit_solution(5425317804277985309)
XLA Ops:
  0.6 0.6 copy-done.6
  1.5 0.7 copy-done.2
  2.2 0.6 copy-done.8
  2.8 0.6 copy-done.7
  3.5 0.7 copy-done.4
  4.4 0.6 copy-done.9
  5.4 1.0 scatter_fusion.1
  6.4 1.0 scatter_fusion
  7.4 80.5 %all_to_all.29 = f32[14,128,2]{0,2,1:T(2,128)S(1)} all-to-all(f32[14,128,2]{0,2,1:T(2,128)S(1)} %bitcast.106), channel_id=1, replica_groups=mesh['groups'=2,'pix'=32,'sub'=4,'rep'=2] {'pix','sub'}, dimensions={1} | all-to-all | bytes 28672 | tf_op jit(solution)/shard_map/all_to_all | solution.py:23
  88.2 1.3 collective-permute-start.1
  89.5 4.6 %collective-permute-start = (f32[7,256]{0,1:T(8,128)S(1)}, f32[7,256]{0,1:T(8,128)S(1)}, u32[]{:S(2)}, u32[]{:S(2)}) collective-permute-start(f32[7,256]{0,1:T(8,128)S(1)} %bitcast.109), channel_id=1, source_target_pairs={{0,8},{8,16},{16,24},{24,32},{32,40},{40,48},{48,56},{56,64},{64,7... | collective-permute-start | bytes 21512 | tf_op jit(solution)/shard_map/ppermute | solution.py:37
  94.1 0.9 collective-permute-done.1
  95.1 1.5 collective-permute-done
  96.7 0.7 broadcast_in_dim.16
  97.4 4.5 %all-to-all-start.1 = ((f32[8,7,768]{2,1,0:T(8,128)}), f32[8,7,768]{2,1,0:T(8,128)S(1)}, u32[]{:S(2)}, u32[]{:S(2)}) async-start(f32[8,7,768]{2,1,0:T(8,128)} %broadcast_in_dim.16), calls=%async_computation.1 | async-start | bytes 393216 | tf_op jit(solution)/shard_map/all_to_all | solution.py:45
  102.0 4.7 %all-to-all-done.1 = f32[8,7,768]{2,1,0:T(8,128)S(1)} async-done(((f32[8,7,768]{2,1,0:T(8,128)}), f32[8,7,768]{2,1,0:T(8,128)S(1)}, u32[]{:S(2)}, u32[]{:S(2)}) %all-to-all-start.1) | async-done | bytes 172064 | tf_op jit(solution)/shard_map/all_to_all | solution.py:45
  106.6 29.2 %while.19 = (s32[]{:T(128)}, f32[3,256]{1,0:T(4,128)S(1)}, f32[48,128]{1,0:T(8,128)S(1)}, f32[7,256]{1,0:T(8,128)S(1)}, f32[48,7,128]{2,1,0:T(8,128)S(1)}, /*index=5*/s32[]{:T(128)}, s32[]{:T(128)}) while((s32[]{:T(128)}, f32[3,256]{1,0:T(4,128)S(1)}, f32[48,128]{1,0:T(8,128)S(1)}, f32[7,256]{1,0:T(8,128)S(1)}, ...), condition=%wide.region_9.10_spmd.clone, body=%wide.region_4.0_spmd.clone.sunk | while | flops 1476739 | bytes 53351 | solution.py:138
  106.6 0.5 fusion.39
  107.3 0.5 fusion.39
  107.9 0.5 fusion.39
  108.5 0.5 fusion.39
  109.1 0.5 fusion.39
  109.7 0.5 fusion.39
  110.3 0.5 fusion.39
  110.9 0.5 fusion.39
  111.5 0.5 fusion.39
  112.1 0.5 fusion.39
  112.7 0.5 fusion.39
  113.3 0.5 fusion.39
  114.0 0.5 fusion.39
  114.6 0.5 fusion.39
  115.2 0.5 fusion.39
  115.8 0.5 fusion.39
  116.4 0.5 fusion.39
  117.0 0.5 fusion.39
  117.6 0.5 fusion.39
  118.2 0.5 fusion.39
  118.8 0.5 fusion.39
  119.4 0.5 fusion.39
  120.1 0.5 fusion.39
  120.7 0.5 fusion.39
  121.3 0.5 fusion.39
  121.9 0.5 fusion.39
  122.5 0.5 fusion.39
  123.1 0.5 fusion.39
  123.7 0.5 fusion.39
  124.3 0.5 fusion.39
  124.9 0.5 fusion.39
  125.5 0.5 fusion.39
  126.1 0.5 fusion.39
  126.8 0.5 fusion.39
  127.4 0.5 fusion.39
  135.8 7.8 %all_to_all.30 = f32[8,1,768]{2,1,0:T(1,128)S(1)} all-to-all(f32[8,1,768]{2,1,0:T(1,128)S(1)} %bitcast.124), channel_id=1, replica_groups=mesh['groups'=2,'pix'=32,'sub'=4,'rep'=2] {'sub','rep'}, dimensions={0} | all-to-all | bytes 49152 | tf_op jit(solution)/shard_map/all_to_all | solution.py:66
  143.7 1.3 collective-permute-start.3
  145.0 5.0 %collective-permute-start.2 = (f32[256]{0:T(256)S(1)}, f32[256]{0:T(256)S(1)}, u32[]{:S(2)}, u32[]{:S(2)}) collective-permute-start(f32[256]{0:T(256)S(1)} %get-tuple-element.202), channel_id=1, source_target_pairs={{0,8},{8,16},{16,24},{24,32},{32,40},{40,48},{48,56},{56,64},{64,7... | collective-permute-start | bytes 3080 | tf_op jit(solution)/shard_map/ppermute | solution.py:73
  150.2 1.1 collective-permute-done.2
  151.5 1.5 copy.55
  153.0 14.9 %all-to-all-start.3 = ((f32[4,128,2]{0,2,1:T(2,128)}), f32[4,128,2]{0,2,1:T(2,128)S(1)}, u32[]{:S(2)}, u32[]{:S(2)}) async-start(f32[4,128,2]{0,2,1:T(2,128)} %copy.55), calls=%async_computation.3 | async-start | bytes 262144 | tf_op jit(solution)/shard_map/all_to_all | solution.py:182
  167.9 28.5 %all-to-all-done.3 = f32[4,128,2]{0,2,1:T(2,128)S(1)} async-done(((f32[4,128,2]{0,2,1:T(2,128)}), f32[4,128,2]{0,2,1:T(2,128)S(1)}, u32[]{:S(2)}, u32[]{:S(2)}) %all-to-all-start.3) | async-done | bytes 4128 | tf_op jit(solution)/shard_map/all_to_all | solution.py:182
  196.4 0.5 slice_reduce_fusion
  197.1 1.8 gather_fusion
  199.0 0.6 gather_fusion.1
  199.7 0.6 copy.56
  200.5 1.8 gather_fusion.2
  (306 shorter events, 12.4 us)
Async XLA Ops:
  0.6 0.7 copy-start.6
  1.5 0.7 copy-start.2
  2.1 0.7 copy-start.8
  2.8 0.7 copy-start.7
  3.5 0.7 copy-start.4
  4.3 0.7 copy-start.9
  4.3 0.8 copy-start.3
  4.3 0.8 copy-start.11
  4.3 0.9 copy-start.10
  4.3 0.9 copy-start.5
  4.4 1.0 copy-start
  4.4 2.0 copy-start.1
  88.2 6.9 %collective-permute-start.1 = (f32[7,256]{0,1:T(8,128)S(1)}, f32[7,256]{0,1:T(8,128)S(1)}, u32[]{:S(2)}, u32[]{:S(2)}) collective-permute-start(f32[7,256]{0,1:T(8,128)S(1)} %bitcast.108), channel_id=1, source_target_pairs={{8,0},{16,8},{24,16},{32,24},{40,32},{48,40},{56,48},{64,56},{72,6... | collective-permute-start | bytes 21512 | tf_op jit(solution)/shard_map/ppermute | solution.py:38
  89.5 7.1 %collective-permute-start = (f32[7,256]{0,1:T(8,128)S(1)}, f32[7,256]{0,1:T(8,128)S(1)}, u32[]{:S(2)}, u32[]{:S(2)}) collective-permute-start(f32[7,256]{0,1:T(8,128)S(1)} %bitcast.109), channel_id=1, source_target_pairs={{0,8},{8,16},{16,24},{24,32},{32,40},{40,48},{48,56},{56,64},{64,7... | collective-permute-start | bytes 21512 | tf_op jit(solution)/shard_map/ppermute | solution.py:37
  97.4 9.3 %all-to-all-start.1 = ((f32[8,7,768]{2,1,0:T(8,128)}), f32[8,7,768]{2,1,0:T(8,128)S(1)}, u32[]{:S(2)}, u32[]{:S(2)}) async-start(f32[8,7,768]{2,1,0:T(8,128)} %broadcast_in_dim.16), calls=%async_computation.1 | async-start | bytes 393216 | tf_op jit(solution)/shard_map/all_to_all | solution.py:45
  143.7 6.5 %collective-permute-start.3 = (f32[256]{0:T(256)S(1)}, f32[256]{0:T(256)S(1)}, u32[]{:S(2)}, u32[]{:S(2)}) collective-permute-start(f32[256]{0:T(256)S(1)} %get-tuple-element.203), channel_id=1, source_target_pairs={{8,0},{16,8},{24,16},{32,24},{40,32},{48,40},{56,48},{64,56},{72,6... | collective-permute-start | bytes 3080 | tf_op jit(solution)/shard_map/ppermute | solution.py:73
  145.0 6.3 %collective-permute-start.2 = (f32[256]{0:T(256)S(1)}, f32[256]{0:T(256)S(1)}, u32[]{:S(2)}, u32[]{:S(2)}) collective-permute-start(f32[256]{0:T(256)S(1)} %get-tuple-element.202), channel_id=1, source_target_pairs={{0,8},{8,16},{16,24},{24,32},{32,40},{40,48},{48,56},{56,64},{64,7... | collective-permute-start | bytes 3080 | tf_op jit(solution)/shard_map/ppermute | solution.py:73
  153.0 43.4 %all-to-all-start.3 = ((f32[4,128,2]{0,2,1:T(2,128)}), f32[4,128,2]{0,2,1:T(2,128)S(1)}, u32[]{:S(2)}, u32[]{:S(2)}) async-start(f32[4,128,2]{0,2,1:T(2,128)} %copy.55), calls=%async_computation.3 | async-start | bytes 262144 | tf_op jit(solution)/shard_map/all_to_all | solution.py:182
where the time goes:
time: 203 us; the launch traced here: 202 us
  blocking collectives  88.3 us (43%)
  waiting for transfers between devices  36.6 us (18%)
  starting transfers between devices  31.7 us (16%)
  other arithmetic  25 us (12%)
  local copies, waits for them, and re-layouts  17.8 us (9%)
    all_to_all x1, blocking collectives, side_by_side(): lax.all_to_all(both, axis, split_axis=split_dim, concat_axis=concat_dim,...  80.5 us
    all_to_all x1, waiting for transfers between devices, shards(): lax.all_to_all(results, ('pix', 'sub'), split_axis=1, concat_axis=1, tile...  28.5 us
    reduce_sum x48, other arithmetic, pair_terms(): jnp.sum(like, axis=0)  23.5 us
    all_to_all x1, starting transfers between devices, shards(): lax.all_to_all(results, ('pix', 'sub'), split_axis=1, concat_axis=1, tile...  14.9 us
    all_to_all x1, blocking collectives, sent_and_summed(): parts = lax.all_to_all(in_blocks(x, dim, size), axis, 0, 0, tiled=True)  7.79 us
    ppermute x2, starting transfers between devices, from_behind(): lax.ppermute(value, axis, [(source, source + steps) for source in range(l...  6.33 us
    all_to_all x1, waiting for transfers between devices, from_everyone(): lax.all_to_all(jnp.broadcast_to(x[None], (size, *x.shape)), axis, 0, 0, t...  4.66 us
    unnamed x26, local copies, waits for them, and re-layouts  4.61 us
  transfers between devices with their start and end apart: 6, of which 5 were waited for; matrix products, arithmetic and copies ran while one was open for 0% of the time, Pallas kernels for 0%

commit v1 on v0

--- a/solution.py
+++ b/solution.py
@@ -1,3 +1,4 @@
+import functools
 import jax
 import jax.numpy as jnp
 from jax import lax
@@ -10,6 +11,21 @@
 empty_wise = -3000.0
 row_offset = 4.0
 inv_two_pi = 0.15915494309189535
+
+
+def screen_choose(base_x, device_axis):
+    return jnp.concatenate(
+        lax.all_to_all(
+            jnp.stack(jnp.split(base_x, lax.axis_size(device_axis), axis=1), axis=0),
+            axis_name=device_axis,
+            split_axis=0,
+            concat_axis=0,
+        ),
+        1,
+    )
+
+
+detail_the_words = functools.partial(screen_choose, device_axis=("pix", "sub"))
 
 
 def side_by_side(arrays, axis, split_dim, concat_dim, along):
@@ -179,7 +195,7 @@
     from_lower = from_behind(wise_part[2 * received :], "pix", 1)
     wise_result = wise_part[received : 2 * received] + from_lower + from_upper
     results = jnp.concatenate([gaia_result, wise_result[None, :]], axis=0)
-    returned = lax.all_to_all(results, ("pix", "sub"), split_axis=1, concat_axis=1, tiled=True)
+    returned = detail_the_words(results)
     return (returned[0][gaia_slot], returned[1:3][:, gaia_slot], returned[3][wise_slot])
 
 

time: 203 us -> 288 us (1.42)
  local copies, waits for them, and re-layouts: 17.8 us -> 101 us
    unnamed x26 -> x153, local copies, waits for them, and re-layouts: 4.61 us -> 77.2 us
    split x0 -> x128, local copies, waits for them, and re-layouts: none -> 11.8 us  [screen_choose(): jnp.split(base_x, lax.axis_size(device_axis), axis=1)]
where the time goes in v1:
time: 288 us; the launch traced here: 287 us
  local copies, waits for them, and re-layouts  101 us (35%)
  blocking collectives  88.3 us (31%)
  waiting for transfers between devices  36.8 us (13%)
  starting transfers between devices  31.7 us (11%)
  other arithmetic  26.8 us (9%)
    all_to_all x1, blocking collectives, side_by_side(): lax.all_to_all(both, axis, split_axis=split_dim, concat_axis=concat_dim,...  80.5 us
    unnamed x153, local copies, waits for them, and re-layouts  77.2 us
    all_to_all x1, waiting for transfers between devices, screen_choose(): lax.all_to_all(jnp.stack(jnp.split(base_x, lax.axis_size(device_axis), ax...  28.5 us
    reduce_sum x48, other arithmetic, pair_terms(): jnp.sum(like, axis=0)  23.5 us
    all_to_all x1, starting transfers between devices, screen_choose(): lax.all_to_all(jnp.stack(jnp.split(base_x, lax.axis_size(device_axis), ax...  14.9 us
    split x128, local copies, waits for them, and re-layouts, screen_choose(): jnp.split(base_x, lax.axis_size(device_axis), axis=1)  11.8 us
    all_to_all x1, blocking collectives, sent_and_summed(): parts = lax.all_to_all(in_blocks(x, dim, size), axis, 0, 0, tiled=True)  7.79 us
    ppermute x2, starting transfers between devices, from_behind(): lax.ppermute(value, axis, [(source, source + steps) for source in range(l...  6.33 us
  transfers between devices with their start and end apart: 6, of which 5 were waited for; matrix products, arithmetic and copies ran while one was open for 0% of the time, Pallas kernels for 0%

profile of v1, /device:TPU:46, one launch (start us, length us, event | category | flops | bytes accessed | tf_op | source)
XLA Modules:
  0.0 287.5 jit_solution(9062337111920642723)
XLA Ops:
  0.6 0.6 copy-done.6
  1.5 0.7 copy-done.2
  2.2 0.6 copy-done.8
  2.8 0.6 copy-done.7
  3.5 0.7 copy-done.4
  5.4 1.0 scatter_fusion.1
  6.4 1.0 scatter_fusion
  7.4 80.5 %all_to_all.28 = f32[14,128,2]{0,2,1:T(2,128)S(1)} all-to-all(f32[14,128,2]{0,2,1:T(2,128)S(1)} %bitcast.388), channel_id=1, replica_groups=mesh['groups'=2,'pix'=32,'sub'=4,'rep'=2] {'pix','sub'}, dimensions={1} | all-to-all | bytes 28672 | tf_op jit(solution)/shard_map/all_to_all | solution.py:39
  88.2 1.3 collective-permute-start.1
  89.5 4.6 %collective-permute-start = (f32[7,256]{0,1:T(8,128)S(1)}, f32[7,256]{0,1:T(8,128)S(1)}, u32[]{:S(2)}, u32[]{:S(2)}) collective-permute-start(f32[7,256]{0,1:T(8,128)S(1)} %bitcast.391), channel_id=1, source_target_pairs={{0,8},{8,16},{16,24},{24,32},{32,40},{40,48},{48,56},{56,64},{64,7... | collective-permute-start | bytes 21512 | tf_op jit(solution)/shard_map/ppermute | solution.py:53
  94.1 0.9 collective-permute-done.1
  95.1 1.5 collective-permute-done
  96.7 0.7 broadcast_in_dim.19
  97.4 4.5 %all-to-all-start.1 = ((f32[8,7,768]{2,1,0:T(8,128)}), f32[8,7,768]{2,1,0:T(8,128)S(1)}, u32[]{:S(2)}, u32[]{:S(2)}) async-start(f32[8,7,768]{2,1,0:T(8,128)} %broadcast_in_dim.19), calls=%async_computation.1 | async-start | bytes 393216 | tf_op jit(solution)/shard_map/all_to_all | solution.py:61
  102.0 4.7 %all-to-all-done.1 = f32[8,7,768]{2,1,0:T(8,128)S(1)} async-done(((f32[8,7,768]{2,1,0:T(8,128)}), f32[8,7,768]{2,1,0:T(8,128)S(1)}, u32[]{:S(2)}, u32[]{:S(2)}) %all-to-all-start.1) | async-done | bytes 172064 | tf_op jit(solution)/shard_map/all_to_all | solution.py:61
  106.6 29.2 %while.19 = (s32[]{:T(128)}, f32[3,256]{1,0:T(4,128)S(1)}, f32[48,128]{1,0:T(8,128)S(1)}, f32[7,256]{1,0:T(8,128)S(1)}, f32[48,7,128]{2,1,0:T(8,128)S(1)}, /*index=5*/s32[]{:T(128)}, s32[]{:T(128)}) while((s32[]{:T(128)}, f32[3,256]{1,0:T(4,128)S(1)}, f32[48,128]{1,0:T(8,128)S(1)}, f32[7,256]{1,0:T(8,128)S(1)}, ...), condition=%wide.region_9.10_spmd.clone, body=%wide.region_4.0_spmd.clone.sunk | while | flops 1476739 | bytes 53351 | solution.py:154
  135.8 7.8 %all_to_all.29 = f32[8,1,768]{2,1,0:T(1,128)S(1)} all-to-all(f32[8,1,768]{2,1,0:T(1,128)S(1)} %bitcast.406), channel_id=1, replica_groups=mesh['groups'=2,'pix'=32,'sub'=4,'rep'=2] {'sub','rep'}, dimensions={0} | all-to-all | bytes 49152 | tf_op jit(solution)/shard_map/all_to_all | solution.py:82
  143.7 1.3 collective-permute-start.3
  145.0 5.0 %collective-permute-start.2 = (f32[256]{0:T(256)S(1)}, f32[256]{0:T(256)S(1)}, u32[]{:S(2)}, u32[]{:S(2)}) collective-permute-start(f32[256]{0:T(256)S(1)} %get-tuple-element.338), channel_id=1, source_target_pairs={{0,8},{8,16},{16,24},{24,32},{32,40},{40,48},{48,56},{56,64},{64,7... | collective-permute-start | bytes 3080 | tf_op jit(solution)/shard_map/ppermute | solution.py:89
  150.0 1.3 collective-permute-done.2
  153.2 0.6 constant_dynamic-update-slice_fusion.127
  169.0 0.6 constant_dynamic-update-slice_fusion.120
  169.6 0.6 constant_dynamic-update-slice_fusion.119
  172.4 0.6 constant_dynamic-update-slice_fusion.114
  175.3 0.6 constant_dynamic-update-slice_fusion.109
  178.1 0.6 constant_dynamic-update-slice_fusion.104
  178.7 0.6 constant_dynamic-update-slice_fusion.103
  179.3 0.6 constant_dynamic-update-slice_fusion.102
  181.0 0.6 constant_dynamic-update-slice_fusion.99
  181.6 0.6 constant_dynamic-update-slice_fusion.98
  183.3 0.6 constant_dynamic-update-slice_fusion.95
  183.9 0.6 constant_dynamic-update-slice_fusion.94
  185.7 0.6 constant_dynamic-update-slice_fusion.91
  186.3 0.6 constant_dynamic-update-slice_fusion.90
  189.1 0.6 constant_dynamic-update-slice_fusion.85
  190.8 0.6 constant_dynamic-update-slice_fusion.82
  193.6 0.6 constant_dynamic-update-slice_fusion.77
  195.4 0.6 constant_dynamic-update-slice_fusion.74
  198.2 0.6 constant_dynamic-update-slice_fusion.69
  198.8 0.6 constant_dynamic-update-slice_fusion.68
  201.1 0.6 constant_dynamic-update-slice_fusion.64
  201.7 0.6 constant_dynamic-update-slice_fusion.63
  204.5 0.6 constant_dynamic-update-slice_fusion.58
  207.4 0.6 constant_dynamic-update-slice_fusion.53
  210.3 0.6 constant_dynamic-update-slice_fusion.48
  210.9 0.6 constant_dynamic-update-slice_fusion.47
  211.5 0.6 constant_dynamic-update-slice_fusion.46
  213.2 0.6 constant_dynamic-update-slice_fusion.43
  216.5 0.6 constant_dynamic-update-slice_fusion.37
  217.1 0.6 constant_dynamic-update-slice_fusion.36
  219.4 0.6 constant_dynamic-update-slice_fusion.32
  221.1 0.6 constant_dynamic-update-slice_fusion.29
  221.7 0.6 constant_dynamic-update-slice_fusion.28
  224.5 0.6 constant_dynamic-update-slice_fusion.23
  225.1 0.6 constant_dynamic-update-slice_fusion.22
  227.4 0.6 constant_dynamic-update-slice_fusion.18
  230.8 0.6 constant_dynamic-update-slice_fusion.12
  236.5 0.6 constant_dynamic-update-slice_fusion.2
  238.2 14.9 %all-to-all-start.3 = ((f32[128,4,2]{1,2,0:T(2,128)}), f32[128,4,2]{1,2,0:T(2,128)S(1)}, u32[]{:S(2)}, u32[]{:S(2)}) async-start(f32[128,4,2]{1,2,0:T(2,128)} %constant_dynamic-update-slice_fusion), calls=%async_computation.3 | async-start | bytes 262144 | tf_op jit(solution)/shard_map/all_to_all | solution.py:18
  253.1 28.5 %all-to-all-done.3 = f32[128,4,2]{1,2,0:T(2,128)S(1)} async-done(((f32[128,4,2]{1,2,0:T(2,128)}), f32[128,4,2]{1,2,0:T(2,128)S(1)}, u32[]{:S(2)}, u32[]{:S(2)}) %all-to-all-start.3) | async-done | bytes 4128 | tf_op jit(solution)/shard_map/all_to_all | solution.py:18
  282.5 1.8 gather_fusion
  284.3 0.6 gather_fusion.1
  284.9 0.6 copy.1216
  285.7 1.8 gather_fusion.2
  (579 shorter events, 94.5 us)
Async XLA Ops:
  0.6 0.7 copy-start.6
  1.5 0.7 copy-start.2
  2.1 0.7 copy-start.8
  2.8 0.7 copy-start.7
  3.5 0.7 copy-start.4
  4.3 0.7 copy-start.9
  4.3 0.8 copy-start.3
  4.3 0.8 copy-start.11
  4.3 0.9 copy-start.10
  4.3 0.9 copy-start.5
  4.4 1.0 copy-start
  4.4 2.0 copy-start.1
  88.2 6.9 %collective-permute-start.1 = (f32[7,256]{0,1:T(8,128)S(1)}, f32[7,256]{0,1:T(8,128)S(1)}, u32[]{:S(2)}, u32[]{:S(2)}) collective-permute-start(f32[7,256]{0,1:T(8,128)S(1)} %bitcast.390), channel_id=1, source_target_pairs={{8,0},{16,8},{24,16},{32,24},{40,32},{48,40},{56,48},{64,56},{72,6... | collective-permute-start | bytes 21512 | tf_op jit(solution)/shard_map/ppermute | solution.py:54
  89.5 7.1 %collective-permute-start = (f32[7,256]{0,1:T(8,128)S(1)}, f32[7,256]{0,1:T(8,128)S(1)}, u32[]{:S(2)}, u32[]{:S(2)}) collective-permute-start(f32[7,256]{0,1:T(8,128)S(1)} %bitcast.391), channel_id=1, source_target_pairs={{0,8},{8,16},{16,24},{24,32},{32,40},{40,48},{48,56},{56,64},{64,7... | collective-permute-start | bytes 21512 | tf_op jit(solution)/shard_map/ppermute | solution.py:53
  97.4 9.3 %all-to-all-start.1 = ((f32[8,7,768]{2,1,0:T(8,128)}), f32[8,7,768]{2,1,0:T(8,128)S(1)}, u32[]{:S(2)}, u32[]{:S(2)}) async-start(f32[8,7,768]{2,1,0:T(8,128)} %broadcast_in_dim.19), calls=%async_computation.1 | async-start | bytes 393216 | tf_op jit(solution)/shard_map/all_to_all | solution.py:61
  143.7 6.4 %collective-permute-start.3 = (f32[256]{0:T(256)S(1)}, f32[256]{0:T(256)S(1)}, u32[]{:S(2)}, u32[]{:S(2)}) collective-permute-start(f32[256]{0:T(256)S(1)} %get-tuple-element.339), channel_id=1, source_target_pairs={{8,0},{16,8},{24,16},{32,24},{40,32},{48,40},{56,48},{64,56},{72,6... | collective-permute-start | bytes 3080 | tf_op jit(solution)/shard_map/ppermute | solution.py:89
  145.0 6.3 %collective-permute-start.2 = (f32[256]{0:T(256)S(1)}, f32[256]{0:T(256)S(1)}, u32[]{:S(2)}, u32[]{:S(2)}) collective-permute-start(f32[256]{0:T(256)S(1)} %get-tuple-element.338), channel_id=1, source_target_pairs={{0,8},{8,16},{16,24},{24,32},{32,40},{40,48},{48,56},{56,64},{64,7... | collective-permute-start | bytes 3080 | tf_op jit(solution)/shard_map/ppermute | solution.py:89
  238.2 43.4 %all-to-all-start.3 = ((f32[128,4,2]{1,2,0:T(2,128)}), f32[128,4,2]{1,2,0:T(2,128)S(1)}, u32[]{:S(2)}, u32[]{:S(2)}) async-start(f32[128,4,2]{1,2,0:T(2,128)} %constant_dynamic-update-slice_fusion), calls=%async_computation.3 | async-start | bytes 262144 | tf_op jit(solution)/shard_map/all_to_all | solution.py:18
